TPU v7x, 128 devices: a whole 4x4x4 slice. The times are simulated.
128 devices in a mesh: layer: 32 (over x_hi, y, z), cuts: 4 (over x_lo, core).
Axes of the slice: x: 4 (x_hi: 2, x_lo: 2; x = x_hi * 2 + x_lo), y: 4, z: 4, core: 2. Of those that a mesh axis runs over, the one named last changes fastest.
Arguments:
- resid: bfloat16 [512, 2, 16384], P(None, None, 'cuts'), may hold values from -6 to 6
- enc_weight: bfloat16 [2, 16384, 8192], P(None, 'cuts', 'layer'), may hold values from -0.03125 to 0.03125
- enc_bias: float32 [8192], P('layer'), may hold values from -1 to 1
- dec_weight: bfloat16 [8192, 2, 16384], P('layer', None, 'cuts'), may hold values from -0.09375 to 0.09375
- dec_bias: float32 [2, 16384], P(None, 'cuts'), may hold values from -1 to 1
Outputs:
- enc_grad: bfloat16 [2, 16384, 8192], P(None, 'cuts', 'layer')
- dec_grad: bfloat16 [8192, 2, 16384], P('layer', None, 'cuts')
All inputs are finite; a program needn't handle non-finite values.
Results may differ from a plain program's by a relative error of at most 0.012.
Values may be sent and summed in bfloat16 or wider, within the bound.
A program may use at most 128 MiB of HBM per device.

v0:
```python
import math
import jax
import jax.numpy as jnp
from jax import lax
from jax.sharding import PartitionSpec as P


def copy_for_each(x, axis):
    copies = jnp.broadcast_to(x, (lax.axis_size(axis), *x.shape))
    return lax.all_to_all(copies, axis, split_axis=0, concat_axis=0, tiled=True)


def taken_together(x, axis):
    everything = copy_for_each(x, axis)
    return jnp.sum(everything, axis=0)


def filled_up(lines, size):
    spare = -len(lines) % size
    return jnp.pad(lines, [(0, spare)] + [(0, 0)] * (lines.ndim - 1))


def sum_by_parts(x, axis):
    lines = x.reshape(-1, *x.shape[1:][-1:])
    padded = filled_up(lines, lax.axis_size(axis))
    own = lax.psum_scatter(padded, axis, scatter_dimension=0, tiled=True)
    whole = lax.all_gather(own, axis, axis=0, tiled=True)
    return whole[: len(lines)].reshape(x.shape)


def per_device(resid, enc_weight, enc_bias, dec_weight, dec_bias):
    rows = resid.shape[0]
    local = resid.reshape(rows, -1)
    width = local.shape[1]
    encoder = enc_weight.reshape(width, -1)
    feats = encoder.shape[1]
    decoder = dec_weight.reshape(feats, width)
    offset = dec_bias.reshape(-1)
    scale = 1.0 / math.sqrt(rows)
    groups = lax.axis_size("layer")
    partial_sum = jnp.dot(local, encoder, preferred_element_type=jnp.float32)
    z_local = taken_together(partial_sum, "cuts") + enc_bias[None, :]
    act = jnp.maximum(z_local, 0.0).astype(jnp.bfloat16)
    share = rows // groups
    block = act
    recon = lax.psum_scatter(
        jnp.dot(block, decoder, preferred_element_type=jnp.float32),
        "layer",
        scatter_dimension=0,
        tiled=True,
    )
    mine = lax.axis_index("layer") * share
    own_rows = lax.dynamic_slice_in_dim(local, mine, share, 0)
    err = (recon + offset[None, :] - own_rows.astype(jnp.float32)).astype(jnp.bfloat16)
    piece = lax.all_gather(err, "layer", axis=0, tiled=True)
    block = act
    grad = lax.dot_general(
        block, piece, (((0,), (0,)), ((), ())), preferred_element_type=jnp.float32
    )
    values = lax.dot_general(
        piece, decoder, (((1,), (1,)), ((), ())), preferred_element_type=jnp.float32
    )
    dact = values
    grad, dact = (grad, dact)
    dec_grad = (grad * scale).astype(jnp.bfloat16)
    back = sum_by_parts(dact, "cuts")
    masked = jnp.where(z_local > 0, back * scale, 0.0).astype(jnp.bfloat16)
    enc_full = lax.dot_general(
        local, masked, (((0,), (0,)), ((), ())), preferred_element_type=jnp.float32
    )
    enc_grad = enc_full.astype(jnp.bfloat16).reshape(enc_weight.shape)
    return (enc_grad, dec_grad.reshape(dec_weight.shape))


def solution(mesh):
    placed = (
        P(None, None, "cuts"),
        P(None, "cuts", "layer"),
        P("layer"),
        P("layer", None, "cuts"),
        P(None, "cuts"),
    )
    return jax.shard_map(
        per_device,
        mesh=mesh,
        in_specs=placed,
        out_specs=(P(None, "cuts", "layer"), P("layer", None, "cuts")),
        check_vma=False,
    )
```

profile of v0, /device:TPU:1, one launch (start us, length us, event | category | flops | bytes accessed | tf_op | source)
XLA Modules:
  0.0 445.2 jit_solution(11260148202417527209)
XLA Ops:
  7.2 9.3 %fusion.4 = f32[512,256]{1,0:T(8,128)S(1)} fusion(bf16[2,4096,256]{2,1,0:T(8,128)(2,1)} %param.6, bf16[512,2,4096]{2,1,0:T(2,128)(2,1)} %param.5), kind=kOutput, calls=%fused_computation.6 | convolution fusion | flops 2147483648 | bytes 13107200 | tf_op jit(solution)/shard_map/dot_general | solution.py:41
  16.5 0.0 copy-start
  16.5 1.5 broadcast_in_dim.6
  18.0 5.0 %all-to-all-start = ((f32[4,512,256]{2,1,0:T(8,128)}), f32[4,512,256]{2,1,0:T(8,128)S(1)}, u32[]{:S(2)}, u32[]{:S(2)}) async-start(f32[4,512,256]{2,1,0:T(8,128)} %broadcast_in_dim.6), calls=%async_computation | async-start | bytes 4194304 | tf_op jit(solution)/shard_map/all_to_all | solution.py:10
  22.9 0.0 reduce-scatter.3.cloned.1.call-start
  22.9 8.7 %copy.12 = bf16[32,8,2,4096]{3,1,2,0:T(8,128)(2,1)} copy(bf16[32,8,2,4096]{3,2,1,0:T(2,128)(2,1)} %bitcast.22) | data formatting | bytes 8388608
  31.6 16.0 %all-to-all-done = f32[4,512,256]{2,1,0:T(8,128)S(1)} async-done(((f32[4,512,256]{2,1,0:T(8,128)}), f32[4,512,256]{2,1,0:T(8,128)S(1)}, u32[]{:S(2)}, u32[]{:S(2)}) %all-to-all-start) | async-done | bytes 2097184 | tf_op jit(solution)/shard_map/all_to_all | solution.py:10
  47.6 0.2 reduce_sum.9
  47.8 0.0 copy-done
  47.8 10.3 %fusion.10 = f32[512,8192]{1,0:T(8,128)} fusion(bf16[256,8192]{1,0:T(8,128)(2,1)} %bitcast.19, f32[512,256]{1,0:T(8,128)S(1)} %reduce_sum.9, f32[256]{0:T(256)S(1)} %copy-done), kind=kOutput, calls=%fused_computation.13 | convolution fusion | flops 2147876864 | bytes 21496832 | tf_op jit(solution)/shard_map/dot_general | solution.py:47
  58.1 0.0 reduce-scatter.3.cloned.1.call-update
  58.1 0.3 all-gather.2.cloned.1.call-start
  58.4 0.0 copy-start.1
  58.4 16.2 %copy.14 = bf16[64,8,2,4096]{3,1,2,0:T(8,128)(2,1)} copy(bf16[64,8,2,4096]{3,2,1,0:T(2,128)(2,1)} %bitcast.21) | data formatting | bytes 16777216
  74.6 0.0 copy-done.1
  74.6 194.2 %reduce-scatter.3.cloned.1.call-done = f32[16,8192]{1,0:T(8,128)} async-done(((f32[512,8192]{1,0:T(8,128)}), f32[16,8192]{1,0:T(8,128)}) %reduce-scatter.3.cloned.1.call-update) | async-done | bytes 524304 | tf_op jit(solution)/shard_map/reduce_scatter | solution.py:46
  268.8 1.9 subtract_convert_fusion
  270.7 0.0 all-gather.2.cloned.1.call-update
  270.7 0.3 reduce-scatter.5.cloned.1.call-start
  271.0 120.5 %all-gather.2.cloned.1.call-done = bf16[512,8192]{1,0:T(8,128)(2,1)} async-done(((bf16[16,8192]{1,0:T(8,128)(2,1)}), bf16[512,8192]{1,0:T(8,128)(2,1)}) %all-gather.2.cloned.1.call-update) | async-done | bytes 8388624 | tf_op jit(solution)/shard_map/all_gather | solution.py:55
  391.6 7.8 %fusion.15 = f32[512,256]{1,0:T(8,128)} fusion(bf16[512,8192]{1,0:T(8,128)(2,1)} %all-gather.2.cloned.1.call-done, bf16[256,8192]{1,0:T(8,128)(2,1)} %bitcast.20), kind=kOutput, calls=%fused_computation.18 | convolution fusion | flops 2147483648 | bytes 13107200 | tf_op jit(solution)/shard_map/dot_general | solution.py:60
  399.3 0.0 reduce-scatter.5.cloned.1.call-update
  399.4 7.8 %fusion = bf16[256,8192]{1,0:T(8,128)(2,1)} fusion(bf16[512,8192]{1,0:T(8,128)(2,1)} %all-gather.2.cloned.1.call-done, f32[512,256]{1,0:T(8,128)S(1)} %reduce_sum.9, f32[256]{0:T(256)S(1)} %copy-done), kind=kOutput, calls=%fused_computation.1 | convolution fusion | flops 2152071168 | bytes 13108224 | tf_op jit(solution)/shard_map/dot_general | solution.py:57
  407.2 7.8 %reshape.22 = bf16[256,2,4096]{2,1,0:T(2,128)(2,1)} reshape(bf16[256,8192]{1,0:T(8,128)(2,1)} %fusion) | data formatting | bytes 8388608 | tf_op jit(solution)/shard_map/reshape | solution.py:72
  415.0 2.1 reduce-scatter.5.cloned.1.call-done
  417.1 7.5 %all_gather.7 = f32[512,256]{1,0:T(8,128)S(1)} all-gather(f32[128,256]{1,0:T(8,128)} %reduce-scatter.5.cloned.1.call-done), channel_id=1, replica_groups=mesh['layer'=32,'cuts'=4] {'cuts'}, dimensions={0}, use_global_device_ids=true | all-gather | bytes 655360 | tf_op jit(solution)/shard_map/all_gather | solution.py:27
  424.5 7.8 %fusion.1 = bf16[8192,256]{0,1:T(8,128)(2,1)} fusion(bf16[512,8192]{1,0:T(8,128)(2,1)} %bitcast.18, f32[512,256]{1,0:T(8,128)S(1)} %all_gather.7, f32[512,256]{1,0:T(8,128)S(1)} %reduce_sum.9, f32[256]{0:T(256)S(1)} %copy-done), kind=kOutput, calls=%fused_computation.3 | convolution fusion | flops 2150236160 | bytes 13632512 | tf_op jit(solution)/shard_map/dot_general | solution.py:68
  432.3 6.4 %copy.11 = bf16[8192,256]{1,0:T(8,128)(2,1)} copy(bf16[8192,256]{0,1:T(8,128)(2,1)} %fusion.1) | data formatting | bytes 8388608
  (1 shorter events, 0.0 us)
Async XLA Ops:
  16.5 31.3 %copy-start = (f32[256]{0:T(256)S(1)}, f32[256]{0:T(256)}, u32[]{:S(2)}) copy-start(f32[256]{0:T(256)} %param.7) | copy-start | bytes 3076
  18.0 29.7 %all-to-all-start = ((f32[4,512,256]{2,1,0:T(8,128)}), f32[4,512,256]{2,1,0:T(8,128)S(1)}, u32[]{:S(2)}, u32[]{:S(2)}) async-start(f32[4,512,256]{2,1,0:T(8,128)} %broadcast_in_dim.6), calls=%async_computation | async-start | bytes 4194304 | tf_op jit(solution)/shard_map/all_to_all | solution.py:10
  22.9 245.9 %reduce-scatter.3.cloned.1.call-start = ((), (), s32[]{:S(2)}) async-start(), calls=%async_computation.3 | async-start | bytes 17301504 | tf_op jit(solution)/shard_map/reduce_scatter | solution.py:46
  58.1 333.4 %all-gather.2.cloned.1.call-start = ((), (), s32[]{:S(2)}) async-start(), calls=%async_computation.4 | async-start | bytes 8650752 | tf_op jit(solution)/shard_map/all_gather | solution.py:55
  58.4 16.2 %copy-start.1 = (f32[2,4096]{1,0:T(2,128)S(1)}, f32[2,4096]{1,0:T(2,128)}, u32[]{:S(2)}) copy-start(f32[2,4096]{1,0:T(2,128)} %param.9) | copy-start | bytes 98308
  270.7 146.3 %reduce-scatter.5.cloned.1.call-start = ((), (), s32[]{:S(2)}) async-start(), calls=%async_computation.5 | async-start | bytes 655360 | tf_op jit(solution)/shard_map/reduce_scatter | solution.py:26
Sparse Core Ops, SparseCore 0:
  58.2 210.5 reduce-scatter.2
  272.6 118.9 all-gather.1
  399.5 17.5 reduce-scatter.4
where the time goes:
time: 446 us; the launch traced here: 445 us
  waiting for transfers between devices  333 us (75%)
  matrix products  42.9 us (10%)
  local copies, waits for them, and re-layouts  40.6 us (9%)
  between operations  13.8 us (3%)
  blocking collectives  7.48 us (2%)
  starting transfers between devices  5.52 us (1%)
    reduce_scatter x1, waiting for transfers between devices, per_device(): lax.psum_scatter(jnp.dot(block, decoder, preferred_element_type=jnp.float...  194 us
    all_gather x1, waiting for transfers between devices, per_device(): piece = lax.all_gather(err, 'layer', axis=0, tiled=True)  121 us
    unnamed x8, local copies, waits for them, and re-layouts  31.3 us
    all_to_all x1, waiting for transfers between devices, copy_for_each(): return lax.all_to_all(copies, axis, split_axis=0, concat_axis=0, tiled=True)  16 us
    dot_general x1, matrix products, per_device(): jnp.dot(block, decoder, preferred_element_type=jnp.float32)  10.3 us
    dot_general x1, matrix products, per_device(): partial_sum = jnp.dot(local, encoder, preferred_element_type=jnp.float32)  9.32 us
  transfers between devices with their start and end apart: 4, of which 4 were waited for; matrix products, arithmetic and copies ran while one was open for 9% of the time, Pallas kernels for 0%

commit v1 on v0

--- a/solution.py
+++ b/solution.py
@@ -52,7 +52,10 @@
     mine = lax.axis_index("layer") * share
     own_rows = lax.dynamic_slice_in_dim(local, mine, share, 0)
     err = (recon + offset[None, :] - own_rows.astype(jnp.float32)).astype(jnp.bfloat16)
-    piece = lax.all_gather(err, "layer", axis=0, tiled=True)
+    count = lax.axis_size("layer")
+    blocks = jnp.stack([err for _ in range(count)])
+    blocks = lax.all_to_all(blocks, "layer", split_axis=0, concat_axis=0)
+    piece = jnp.concatenate(blocks, axis=0)
     block = act
     grad = lax.dot_general(
         block, piece, (((0,), (0,)), ((), ())), preferred_element_type=jnp.float32

time: 446 us -> 426 us (0.955)
  waiting for transfers between devices: 333 us -> 243 us
  blocking collectives: 7.48 us -> 78.6 us
  matrix products: 42.9 us -> 38.3 us
    all_gather x1 -> x0, waiting for transfers between devices: 121 us -> none  [per_device(): piece = lax.all_gather(err, 'layer', axis=0, tiled=True)]
    all_to_all x0 -> x1, blocking collectives: none -> 71.1 us  [per_device(): blocks = lax.all_to_all(blocks, 'layer', split_axis=0, concat_axis=0)]
    reduce_scatter x1, waiting for transfers between devices: 2.08 us -> 32.7 us  [sum_by_parts(): own = lax.psum_scatter(padded, axis, scatter_dimension=0, tiled=True)]
    dot_general x1, matrix products: 7.78 us -> 3.19 us  [per_device(): lax.dot_general(piece, decoder, (((1,), (1,)), ((), ())), preferred_eleme...]
    unnamed x8 -> x12, local copies, waits for them, and re-layouts: 31.3 us -> 34.5 us
  transfers between devices with their start and end apart: 4 -> 3, of which waited for: 4 -> 3; matrix products, arithmetic and copies ran while one was open for 9% -> 10% of each run, Pallas kernels for 0% -> 0%
where the time goes in v1:
time: 426 us; the launch traced here: 425 us
  waiting for transfers between devices  243 us (57%)
  blocking collectives  78.6 us (18%)
  local copies, waits for them, and re-layouts  44.8 us (11%)
  matrix products  38.3 us (9%)
  between operations  14.1 us (3%)
  starting transfers between devices  5.22 us (1%)
    reduce_scatter x1, waiting for transfers between devices, per_device(): lax.psum_scatter(jnp.dot(block, decoder, preferred_element_type=jnp.float...  194 us
    all_to_all x1, blocking collectives, per_device(): blocks = lax.all_to_all(blocks, 'layer', split_axis=0, concat_axis=0)  71.1 us
    unnamed x12, local copies, waits for them, and re-layouts  34.5 us
    reduce_scatter x1, waiting for transfers between devices, sum_by_parts(): own = lax.psum_scatter(padded, axis, scatter_dimension=0, tiled=True)  32.7 us
    all_to_all x1, waiting for transfers between devices, copy_for_each(): return lax.all_to_all(copies, axis, split_axis=0, concat_axis=0, tiled=True)  16 us
    dot_general x1, matrix products, per_device(): jnp.dot(block, decoder, preferred_element_type=jnp.float32)  10.3 us
    dot_general x1, matrix products, per_device(): partial_sum = jnp.dot(local, encoder, preferred_element_type=jnp.float32)  9.32 us
  transfers between devices with their start and end apart: 3, of which 3 were waited for; matrix products, arithmetic and copies ran while one was open for 10% of the time, Pallas kernels for 0%

profile of v1, /device:TPU:1, one launch (start us, length us, event | category | flops | bytes accessed | tf_op | source)
XLA Modules:
  0.0 425.3 jit_solution(1135299239164200467)
XLA Ops:
  7.2 9.3 %fusion.4 = f32[512,256]{1,0:T(8,128)S(1)} fusion(bf16[2,4096,256]{2,1,0:T(8,128)(2,1)} %param.6, bf16[512,2,4096]{2,1,0:T(2,128)(2,1)} %param.5), kind=kOutput, calls=%fused_computation.6 | convolution fusion | flops 2147483648 | bytes 13107200 | tf_op jit(solution)/shard_map/dot_general | solution.py:41
  16.5 0.0 copy-start.2
  16.5 1.5 broadcast_in_dim.6
  18.0 5.0 %all-to-all-start = ((f32[4,512,256]{2,1,0:T(8,128)}), f32[4,512,256]{2,1,0:T(8,128)S(1)}, u32[]{:S(2)}, u32[]{:S(2)}) async-start(f32[4,512,256]{2,1,0:T(8,128)} %broadcast_in_dim.6), calls=%async_computation | async-start | bytes 4194304 | tf_op jit(solution)/shard_map/all_to_all | solution.py:10
  22.9 0.0 reduce-scatter.3.cloned.1.call-start
  22.9 8.7 %copy.12 = bf16[32,8,2,4096]{3,1,2,0:T(8,128)(2,1)} copy(bf16[32,8,2,4096]{3,2,1,0:T(2,128)(2,1)} %bitcast.25) | data formatting | bytes 8388608
  31.6 16.0 %all-to-all-done = f32[4,512,256]{2,1,0:T(8,128)S(1)} async-done(((f32[4,512,256]{2,1,0:T(8,128)}), f32[4,512,256]{2,1,0:T(8,128)S(1)}, u32[]{:S(2)}, u32[]{:S(2)}) %all-to-all-start) | async-done | bytes 2097184 | tf_op jit(solution)/shard_map/all_to_all | solution.py:10
  47.6 0.2 reduce_sum.9
  47.8 0.0 copy-done.2
  47.8 10.3 %fusion.10 = f32[512,8192]{1,0:T(8,128)} fusion(bf16[256,8192]{1,0:T(8,128)(2,1)} %bitcast.22, f32[512,256]{1,0:T(8,128)S(1)} %reduce_sum.9, f32[256]{0:T(256)S(1)} %copy-done.2), kind=kOutput, calls=%fused_computation.13 | convolution fusion | flops 2147876864 | bytes 21496832 | tf_op jit(solution)/shard_map/dot_general | solution.py:47
  58.1 0.0 reduce-scatter.3.cloned.1.call-update
  58.1 0.3 reduce-scatter.5.cloned.1.call-start
  58.4 0.0 copy-start.3
  58.4 16.2 %copy.14 = bf16[64,8,2,4096]{3,1,2,0:T(8,128)(2,1)} copy(bf16[64,8,2,4096]{3,2,1,0:T(2,128)(2,1)} %bitcast.24) | data formatting | bytes 16777216
  74.6 0.0 copy-done.3
  74.6 194.2 %reduce-scatter.3.cloned.1.call-done = f32[16,8192]{1,0:T(8,128)} async-done(((f32[512,8192]{1,0:T(8,128)}), f32[16,8192]{1,0:T(8,128)}) %reduce-scatter.3.cloned.1.call-update) | async-done | bytes 524304 | tf_op jit(solution)/shard_map/reduce_scatter | solution.py:46
  268.8 1.2 subtract_convert_fusion
  270.0 1.0 stack.2
  271.0 0.0 copy-start.1
  271.0 71.1 %all_to_all.10 = bf16[32,16,8192]{2,1,0:T(8,128)(2,1)S(1)} all-to-all(bf16[32,16,8192]{2,1,0:T(8,128)(2,1)S(1)} %stack.2), channel_id=1, replica_groups=mesh['layer'=32,'cuts'=4] {'layer'}, dimensions={0} | all-to-all | bytes 16777216 | tf_op jit(solution)/shard_map/all_to_all | solution.py:57
  342.2 0.0 copy-start
  342.2 3.2 copy-done
  345.4 0.0 copy-done.1
  345.4 3.2 fusion.15
  348.6 0.0 reduce-scatter.5.cloned.1.call-update
  348.6 7.8 %fusion = bf16[256,8192]{1,0:T(8,128)(2,1)} fusion(bf16[512,8192]{1,0:T(8,128)(2,1)} %bitcast.21, f32[512,256]{1,0:T(8,128)S(1)} %reduce_sum.9, f32[256]{0:T(256)S(1)} %copy-done.2), kind=kOutput, calls=%fused_computation.1 | convolution fusion | flops 2152071168 | bytes 13108224 | tf_op jit(solution)/shard_map/dot_general | solution.py:60
  356.4 7.8 %reshape.28 = bf16[256,2,4096]{2,1,0:T(2,128)(2,1)} reshape(bf16[256,8192]{1,0:T(8,128)(2,1)} %fusion) | data formatting | bytes 8388608 | tf_op jit(solution)/shard_map/reshape | solution.py:75
  364.2 32.7 %reduce-scatter.5.cloned.1.call-done = f32[128,256]{1,0:T(8,128)} async-done(((f32[512,256]{1,0:T(8,128)}), f32[128,256]{1,0:T(8,128)}) %reduce-scatter.5.cloned.1.call-update) | async-done | bytes 131088 | tf_op jit(solution)/shard_map/reduce_scatter | solution.py:26
  396.9 7.5 %all_gather.3 = f32[512,256]{1,0:T(8,128)S(1)} all-gather(f32[128,256]{1,0:T(8,128)} %reduce-scatter.5.cloned.1.call-done), channel_id=1, replica_groups=mesh['layer'=32,'cuts'=4] {'cuts'}, dimensions={0}, use_global_device_ids=true | all-gather | bytes 655360 | tf_op jit(solution)/shard_map/all_gather | solution.py:27
  404.4 7.8 %fusion.1 = bf16[8192,256]{0,1:T(8,128)(2,1)} fusion(bf16[512,8192]{1,0:T(8,128)(2,1)} %bitcast.19, f32[512,256]{1,0:T(8,128)S(1)} %all_gather.3, f32[512,256]{1,0:T(8,128)S(1)} %reduce_sum.9, f32[256]{0:T(256)S(1)} %copy-done.2), kind=kOutput, calls=%fused_computation.3 | convolution fusion | flops 2150236160 | bytes 13632512 | tf_op jit(solution)/shard_map/dot_general | solution.py:71
  412.1 6.4 %copy.11 = bf16[8192,256]{1,0:T(8,128)(2,1)} copy(bf16[8192,256]{0,1:T(8,128)(2,1)} %fusion.1) | data formatting | bytes 8388608
  (1 shorter events, 0.0 us)
Async XLA Ops:
  16.5 31.3 %copy-start.2 = (f32[256]{0:T(256)S(1)}, f32[256]{0:T(256)}, u32[]{:S(2)}) copy-start(f32[256]{0:T(256)} %param.7) | copy-start | bytes 3076
  18.0 29.7 %all-to-all-start = ((f32[4,512,256]{2,1,0:T(8,128)}), f32[4,512,256]{2,1,0:T(8,128)S(1)}, u32[]{:S(2)}, u32[]{:S(2)}) async-start(f32[4,512,256]{2,1,0:T(8,128)} %broadcast_in_dim.6), calls=%async_computation | async-start | bytes 4194304 | tf_op jit(solution)/shard_map/all_to_all | solution.py:10
  22.9 245.9 %reduce-scatter.3.cloned.1.call-start = ((), (), s32[]{:S(2)}) async-start(), calls=%async_computation.4 | async-start | bytes 17301504 | tf_op jit(solution)/shard_map/reduce_scatter | solution.py:46
  58.1 338.8 %reduce-scatter.5.cloned.1.call-start = ((), (), s32[]{:S(2)}) async-start(), calls=%async_computation.5 | async-start | bytes 655360 | tf_op jit(solution)/shard_map/reduce_scatter | solution.py:26
  58.4 16.2 %copy-start.3 = (f32[2,4096]{1,0:T(2,128)S(1)}, f32[2,4096]{1,0:T(2,128)}, u32[]{:S(2)}) copy-start(f32[2,4096]{1,0:T(2,128)} %param.9) | copy-start | bytes 98308
  271.0 74.4 %copy-start.1 = (bf16[32,8,2,4096]{3,1,2,0:T(8,128)(2,1)S(1)}, bf16[32,8,2,4096]{3,1,2,0:T(8,128)(2,1)}, u32[]{:S(2)}) copy-start(bf16[32,8,2,4096]{3,1,2,0:T(8,128)(2,1)} %copy.12) | copy-start | bytes 12582916
  342.2 3.2 copy-start
Sparse Core Ops, SparseCore 0:
  58.2 210.5 reduce-scatter.2
  348.7 48.1 reduce-scatter.4
